TPU v7x, 256 devices: a whole 4x4x8 slice. The times are simulated.
256 devices in a mesh: actor: 32 (over z, x), mp: 8 (over y, core).
Axes of the slice: x: 4, y: 4, z: 8, core: 2. Of those that a mesh axis runs over, the one named last changes fastest.
Arguments:
- resid: bfloat16 [32768, 4096], P('actor')
- norm_gain: bfloat16 [4096], replicated, may hold values from 0.25 to 1.75
- query_weight: bfloat16 [4096, 4096], P(None, 'mp'), may hold values from -0.09375 to 0.09375
- cotangent: bfloat16 [32768, 4096], P('actor', 'mp'), may hold values from -1.25 to 1.25
- lengths: int32 [128], P('actor'), may hold values from 1 to 256
- owner: int32 [32], replicated, may hold values from 0 to 31, each once
- adapter_table: float32 [8, 32, 16, 128], P('mp', 'actor')
- moment_one: float32 [8, 32, 16, 128], P('mp', 'actor'), may hold values from -3 to 3
- moment_two: float32 [8, 32, 16, 128], P('mp', 'actor'), may hold values from 0.003 to 0.1
Outputs:
- query: bfloat16 [32768, 4096], P('actor', 'mp')
- adapter_new: float32 [8, 32, 16, 128], P('mp', 'actor')
- moment_one_new: float32 [8, 32, 16, 128], P('mp', 'actor')
- moment_two_new: float32 [8, 32, 16, 128], P('mp', 'actor')
- merged: bfloat16 [4096, 4096], P('actor', 'mp')
Inputs may be any that keep to these rules, and one draw needn't show every extreme that they name: owner is a permutation: every actor keeps exactly one block of each feature slice.
All inputs are finite; a program needn't handle non-finite values.
Results may differ from a plain program's by a relative error of at most 0.0064.
Values may be sent and summed in bfloat16 or wider, within the bound.
No kernel may reach another device: no remote copies, remote signals or barrier semaphores. Data moves between devices by JAX's collectives and lax.ppermute only.
A program may use at most 128 MiB of HBM per device.

v0:
```python
import jax
import jax.numpy as jnp
from jax import lax
from jax.sharding import PartitionSpec as P

LEN = 256


adapter_scale = 0.5
learn_rate = 0.003
beta_one = 0.9
beta_two = 0.999
fix_one = 1.0 - 0.9**10
fix_two = 1.0 - 0.999**10


def from_everyone(x, axis):
    size = lax.axis_size(axis)
    return lax.all_to_all(jnp.broadcast_to(x[None], (size, *x.shape)), axis, 0, 0, tiled=True)


def joined_along(pieces, dim):
    shape = list(pieces.shape[1:])
    shape[dim] *= pieces.shape[0]
    return jnp.moveaxis(pieces, 0, dim).reshape(shape)


def gather_directly(x, axis, dim):
    pieces = from_everyone(x, axis)
    return joined_along(pieces, dim)


def over_copies(x, axis):
    return from_everyone(x, axis).sum(axis=0)


def together(arrays, axis):
    ends = [0]
    for a in arrays:
        ends.append(ends[-1] + a.size)
    subtotal = over_copies(jnp.concatenate([a.ravel() for a in arrays]), axis)
    return tuple((subtotal[b:e].reshape(a.shape) for a, b, e in zip(arrays, ends, ends[1:])))


def cut_along(x, dim, size):
    shape = x.shape
    pieces = x.reshape(*shape[:dim], size, shape[dim] // size, *shape[dim + 1 :])
    return jnp.moveaxis(pieces, dim, 0)


def sent_and_summed(x, axis, dim):
    size = lax.axis_size(axis)
    pieces = lax.all_to_all(cut_along(x, dim, size), axis, 0, 0, tiled=True)
    return jnp.sum(pieces, axis=0)


def broadcast(x, axis, root):
    return lax.dynamic_index_in_dim(lax.all_gather(x, axis), root, 0, keepdims=False)


def contracted_rows(left, right):
    return lax.dot_general(
        left, right, (((0,), (0,)), ((), ())), preferred_element_type=jnp.float32
    )


def contracted_columns(left, right):
    return lax.dot_general(
        left, right, (((1,), (1,)), ((), ())), preferred_element_type=jnp.float32
    )


def slice_rows(gathered, owner, n_actor):
    block = gathered.shape[0] // n_actor
    ordered = jnp.take(gathered.reshape(n_actor, block, gathered.shape[1]), owner, axis=0)
    return ordered.reshape(n_actor * block, gathered.shape[1])


def body(
    resid, norm_gain, query_weight, cotangent, lengths, owner, adapter_table, moment_one, moment_two
):
    n_actor = lax.axis_size("actor")
    n_mp = lax.axis_size("mp")
    mp_index = lax.axis_index("mp")
    actor_index = lax.axis_index("actor")
    tokens = resid.shape[0]
    width = resid.shape[1]
    cols = query_weight.shape[1]
    block = adapter_table.shape[2]
    rank = adapter_table.shape[3] // 2
    stream = resid.astype(jnp.float32)
    meansq = jnp.mean(stream * stream, axis=1, keepdims=True)
    normalized_input = (
        stream * lax.rsqrt(meansq + 1e-05) * norm_gain.astype(jnp.float32)[None, :]
    ).astype(jnp.bfloat16)
    index = jnp.arange(tokens, dtype=jnp.int32)
    position = index % LEN
    sequence = index // LEN
    seq_ids = jnp.arange(lengths.shape[0], dtype=jnp.int32)
    active_rows = jnp.any(
        (sequence[:, None] == seq_ids[None, :]) & (position[:, None] < lengths[None, :]), axis=1
    )
    masked_rows = jnp.where(active_rows[:, None], cotangent, jnp.zeros_like(cotangent))
    normalized_local = lax.dynamic_slice_in_dim(normalized_input, mp_index * cols, cols, 1)
    now_shard = adapter_table.reshape(block, 2 * rank).astype(jnp.bfloat16)
    part = gather_directly(now_shard, "actor", 0)
    mine = slice_rows(part, owner, n_actor)
    bt_mine = mine[:, rank:]
    low_part = jnp.dot(normalized_local, mine[:, :rank], preferred_element_type=jnp.float32)
    back_part = jnp.dot(masked_rows, bt_mine, preferred_element_type=jnp.float32)
    low_sum, back_sum = together((low_part.reshape(-1, 128), back_part.reshape(-1, 128)), "mp")
    low_full = low_sum.reshape(tokens, rank)
    back_full = back_sum.reshape(tokens, rank)
    lowrank_output = low_full.astype(jnp.bfloat16)
    backward_rows = back_full.astype(jnp.bfloat16)
    base_output = jnp.dot(normalized_input, query_weight, preferred_element_type=jnp.float32)
    extra_term = contracted_columns(lowrank_output, bt_mine)
    query = jnp.where(active_rows[:, None], base_output + adapter_scale * extra_term, 0.0).astype(
        jnp.bfloat16
    )
    down_gradient = adapter_scale * contracted_rows(normalized_local, backward_rows)
    up_transposed_gradient = adapter_scale * contracted_rows(masked_rows, lowrank_output)
    grad = jnp.concatenate([down_gradient, up_transposed_gradient], axis=1)
    actors = jnp.arange(n_actor, dtype=jnp.int32)
    inverse = jnp.sum(jnp.where(owner[None, :] == actors[:, None], actors[None, :], 0), axis=1)
    reordered = jnp.take(grad.reshape(n_actor, block, 2 * rank), inverse, axis=0).reshape(
        cols, 2 * rank
    )
    summed = sent_and_summed(reordered, "actor", 0)
    first = beta_one * moment_one.reshape(block, 2 * rank) + (1.0 - beta_one) * summed
    second = beta_two * moment_two.reshape(block, 2 * rank) + (1.0 - beta_two) * summed * summed
    updated = adapter_table.reshape(block, 2 * rank) - learn_rate * (first / fix_one) / (
        jnp.sqrt(second / fix_two) + 1e-08
    )
    updated_low = updated.astype(jnp.bfloat16)
    row_count = width // n_actor
    fresh_part = gather_directly(updated_low, "actor", 0)
    fresh_mine = slice_rows(fresh_part, owner, n_actor)
    up_transposed_columns = fresh_mine[:, rank:]
    ratio = n_actor // n_mp
    offered = lax.dynamic_slice_in_dim(fresh_mine, actor_index % ratio * row_count, row_count, 0)[
        :, :rank
    ]
    down_matrix_rows = broadcast(offered, "mp", actor_index // ratio)
    weight_rows = lax.dynamic_slice_in_dim(query_weight, actor_index * row_count, row_count, 0)
    merged = (
        weight_rows.astype(jnp.float32)
        + adapter_scale * contracted_columns(down_matrix_rows, up_transposed_columns)
    ).astype(jnp.bfloat16)
    shape = adapter_table.shape
    return (query, updated.reshape(shape), first.reshape(shape), second.reshape(shape), merged)


def solution(mesh):
    return jax.shard_map(
        body,
        mesh=mesh,
        in_specs=(
            P("actor", None),
            P(),
            P(None, "mp"),
            P("actor", "mp"),
            P("actor"),
            P(),
            P("mp", "actor", None, None),
            P("mp", "actor", None, None),
            P("mp", "actor", None, None),
        ),
        out_specs=(
            P("actor", "mp"),
            P("mp", "actor", None, None),
            P("mp", "actor", None, None),
            P("mp", "actor", None, None),
            P("actor", "mp"),
        ),
        check_vma=False,
    )
```

profile of v0, /device:TPU:1, one launch (start us, length us, event | category | flops | bytes accessed | tf_op | source)
XLA Modules:
  0.0 157.1 jit_solution(17879130552289466614)
XLA Ops:
  0.6 0.7 bitcast_convert_fusion
  1.3 0.7 broadcast_in_dim.82
  2.0 11.9 %all-to-all-start = ((bf16[32,16,128]{2,1,0:T(8,128)(2,1)}), bf16[32,16,128]{2,1,0:T(8,128)(2,1)S(1)}, u32[]{:S(2)}, u32[]{:S(2)}) async-start(bf16[32,16,128]{2,1,0:T(8,128)(2,1)} %broadcast_in_dim.82), calls=%async_computation | async-start | bytes 262144 | tf_op jit(solution)/shard_map/all_to_all | solution.py:19
  13.9 0.7 compare_select_fusion
  14.5 0.7 convert_element_type.41
  15.2 5.1 %fusion = f32[1024]{0:T(1024)S(1)} fusion(bf16[1024,4096]{1,0:T(8,128)(2,1)} %param.11), kind=kLoop, calls=%fused_computation.5 | loop fusion | flops 12581888 | bytes 8392704 | tf_op jit(solution)/shard_map/reduce_sum | solution.py:92
  20.4 10.4 %fusion.2 = bf16[1024,4096]{1,0:T(8,128)(2,1)} fusion(bf16[1024,4096]{1,0:T(8,128)(2,1)} %param.11, f32[4096]{0:T(1024)S(1)} %convert_element_type.41, f32[1024]{0:T(1024)S(1)} %add_rsqrt_fusion), kind=kLoop, calls=%fused_computation.7 | loop fusion | flops 16777216 | bytes 16797696 | tf_op jit(solution)/shard_map/convert_element_type | solution.py:95
  31.6 1.7 %fusion.6 = f32[1024,64]{1,0:T(8,128)S(1)} fusion(bf16[1024,4096]{1,0:T(8,128)(2,1)} %fusion.2, s32[]{:T(128)S(6)} %select_n.83, bf16[512,128]{1,0:T(8,128)(2,1)S(1)} %bitcast.40), kind=kOutput, calls=%fused_computation.16 | convolution fusion | flops 67108864 | bytes 1441796 | tf_op jit(solution)/shard_map/dot_general | solution.py:109
  34.2 4.1 %broadcast_in_dim.84 = f32[8,1,131072]{2,1,0:T(1,128)} broadcast(f32[131072]{0:T(1024)S(1)} %pad_maximum_fusion), dimensions={2} | broadcast | bytes 4718592 | tf_op jit(solution)/shard_map/broadcast_in_dim | solution.py:19
  38.3 5.4 %all-to-all-start.1 = ((f32[8,1,131072]{2,1,0:T(1,128)}), f32[8,1,131072]{2,1,0:T(1,128)}, u32[]{:S(2)}, u32[]{:S(2)}) async-start(f32[8,1,131072]{2,1,0:T(1,128)} %broadcast_in_dim.84), calls=%async_computation.1 | async-start | bytes 8388608 | tf_op jit(solution)/shard_map/all_to_all | solution.py:19
  43.8 48.7 %all-to-all-done.1 = f32[8,1,131072]{2,1,0:T(1,128)} async-done(((f32[8,1,131072]{2,1,0:T(1,128)}), f32[8,1,131072]{2,1,0:T(1,128)}, u32[]{:S(2)}, u32[]{:S(2)}) %all-to-all-start.1) | async-done | bytes 4194336 | tf_op jit(solution)/shard_map/all_to_all | solution.py:19
  92.5 5.3 %reduce_sum.41 = bf16[131072]{0:T(1024)(128)(2,1)S(1)} reduce(f32[8,1,131072]{2,1,0:T(1,128)} %all-to-all-done.1, f32[]{:T(128)} %constant.108.clone.1), dimensions={0,1}, to_apply=%region_2.4 | reduce | flops 917504 | bytes 4456452 | tf_op jit(solution)/shard_map/reduce_sum | solution.py:34
  97.9 1.6 %convolution_multiply_fusion.2 = f32[512,64]{0,1:T(8,128)S(1)} fusion(bf16[1024,64]{1,0:T(8,128)(2,1)S(1)} %convert_element_type.46, bf16[1024,4096]{1,0:T(8,128)(2,1)} %fusion.2, s32[]{:T(128)S(6)} %select_n.83), kind=kOutput, calls=%fused_computation.13 | convolution fusion | flops 67141632 | bytes 1310724 | tf_op jit(solution)/shard_map/dot_general | solution.py:62
  100.9 0.8 broadcast_select_fusion.3
  101.7 9.5 %all-to-all-start.2 = ((f32[32,16,128]{2,1,0:T(8,128)}), f32[32,16,128]{2,1,0:T(8,128)S(1)}, u32[]{:S(2)}, u32[]{:S(2)}) async-start(f32[32,16,128]{2,1,0:T(8,128)} %broadcast_select_fusion.3), calls=%async_computation.2 | async-start | bytes 524288 | tf_op jit(solution)/shard_map/all_to_all | solution.py:53
  111.2 8.2 %fusion.43 = f32[1024,512]{1,0:T(8,128)S(1)} fusion(bf16[1024,4096]{1,0:T(8,128)(2,1)} %fusion.2, bf16[4096,512]{1,0:T(8,128)(2,1)} %param.13), kind=kOutput, calls=%fused_computation.78 | convolution fusion | flops 4294967296 | bytes 14680064 | tf_op jit(solution)/shard_map/dot_general | solution.py:116
  119.4 2.8 %all-to-all-done.2 = f32[32,16,128]{2,1,0:T(8,128)S(1)} async-done(((f32[32,16,128]{2,1,0:T(8,128)}), f32[32,16,128]{2,1,0:T(8,128)S(1)}, u32[]{:S(2)}, u32[]{:S(2)}) %all-to-all-start.2) | async-done | bytes 262176 | tf_op jit(solution)/shard_map/all_to_all | solution.py:53
  122.4 0.7 broadcast_in_dim.90
  123.0 6.4 %all-to-all-start.3 = ((bf16[32,16,128]{2,1,0:T(8,128)(2,1)}), bf16[32,16,128]{2,1,0:T(8,128)(2,1)S(1)}, u32[]{:S(2)}, u32[]{:S(2)}) async-start(bf16[32,16,128]{2,1,0:T(8,128)(2,1)} %broadcast_in_dim.90), calls=%async_computation.3 | async-start | bytes 262144 | tf_op jit(solution)/shard_map/all_to_all | solution.py:19
  129.4 1.5 select_convert_fusion
  130.9 0.6 divide_subtract_fusion
  131.6 7.2 %all-to-all-done.3 = bf16[32,16,128]{2,1,0:T(8,128)(2,1)S(1)} async-done(((bf16[32,16,128]{2,1,0:T(8,128)(2,1)}), bf16[32,16,128]{2,1,0:T(8,128)(2,1)S(1)}, u32[]{:S(2)}, u32[]{:S(2)}) %all-to-all-start.3) | async-done | bytes 131104 | tf_op jit(solution)/shard_map/all_to_all | solution.py:19
  139.5 15.8 %all-gather = bf16[1024,64]{1,0:T(8,128)(2,1)S(1)} all-gather(bf16[128,64]{1,0:T(8,128)(2,1)S(1)} %constant_dynamic-slice_fusion), channel_id=2, replica_groups=mesh['actor'=32,'mp'=8] {'mp'}, dimensions={0}, use_global_device_ids=true | all-gather | bytes 147456 | tf_op jit(solution)/shard_map/all_gather | solution.py:58
  155.3 1.8 %fusion.4 = bf16[128,512]{1,0:T(8,128)(2,1)} fusion(bf16[512,128]{1,0:T(8,128)(2,1)S(1)} %bitcast.45, bf16[4096,512]{1,0:T(8,128)(2,1)} %param.13, s32[]{:T(128)S(6)} %select_n.90, bf16[8,128,64]{2,1,0:T(8,128)(2,1)S(1)} %bitcast.46, s32[]{:T(128)S(6)} %select_n.94), kind=kOutput, calls=%fused_computation.11 | convolution fusion | flops 8650752 | bytes 425992 | tf_op jit(solution)/shard_map/dot_general | solution.py:68
  (40 shorter events, 4.1 us)
Async XLA Ops:
  2.0 28.9 %all-to-all-start = ((bf16[32,16,128]{2,1,0:T(8,128)(2,1)}), bf16[32,16,128]{2,1,0:T(8,128)(2,1)S(1)}, u32[]{:S(2)}, u32[]{:S(2)}) async-start(bf16[32,16,128]{2,1,0:T(8,128)(2,1)} %broadcast_in_dim.82), calls=%async_computation | async-start | bytes 262144 | tf_op jit(solution)/shard_map/all_to_all | solution.py:19
  20.3 10.5 %copy-start.3 = (s32[4]{0:T(128)S(1)}, s32[4]{0:T(128)}, u32[]{:S(2)}) copy-start(s32[4]{0:T(128)} %param.15) | copy-start | bytes 52
  20.3 10.6 %copy-start.5 = (s32[32]{0:T(128)S(1)}, s32[32]{0:T(128)}, u32[]{:S(2)}) copy-start(s32[32]{0:T(128)} %param.16) | copy-start | bytes 388
  20.3 13.1 %copy-start.4 = (bf16[1024,512]{1,0:T(8,128)(2,1)S(1)}, bf16[1024,512]{1,0:T(8,128)(2,1)}, u32[]{:S(2)}) copy-start(bf16[1024,512]{1,0:T(8,128)(2,1)} %param.14) | copy-start | bytes 3145732
  38.3 54.2 %all-to-all-start.1 = ((f32[8,1,131072]{2,1,0:T(1,128)}), f32[8,1,131072]{2,1,0:T(1,128)}, u32[]{:S(2)}, u32[]{:S(2)}) async-start(f32[8,1,131072]{2,1,0:T(1,128)} %broadcast_in_dim.84), calls=%async_computation.1 | async-start | bytes 8388608 | tf_op jit(solution)/shard_map/all_to_all | solution.py:19
  101.7 20.6 %all-to-all-start.2 = ((f32[32,16,128]{2,1,0:T(8,128)}), f32[32,16,128]{2,1,0:T(8,128)S(1)}, u32[]{:S(2)}, u32[]{:S(2)}) async-start(f32[32,16,128]{2,1,0:T(8,128)} %broadcast_select_fusion.3), calls=%async_computation.2 | async-start | bytes 524288 | tf_op jit(solution)/shard_map/all_to_all | solution.py:53
  111.2 11.1 %copy-start = (f32[1,1,16,128]{3,2,1,0:T(8,128)S(1)}, f32[1,1,16,128]{3,2,1,0:T(8,128)}, u32[]{:S(2)}) copy-start(f32[1,1,16,128]{3,2,1,0:T(8,128)} %param.17) | copy-start | bytes 24580
  111.2 11.1 %copy-start.1 = (f32[1,1,16,128]{3,2,1,0:T(8,128)S(1)}, f32[1,1,16,128]{3,2,1,0:T(8,128)}, u32[]{:S(2)}) copy-start(f32[1,1,16,128]{3,2,1,0:T(8,128)} %param.18) | copy-start | bytes 24580
  111.2 11.1 %copy-start.2 = (f32[1,1,16,128]{3,2,1,0:T(8,128)S(1)}, f32[1,1,16,128]{3,2,1,0:T(8,128)}, u32[]{:S(2)}) copy-start(f32[1,1,16,128]{3,2,1,0:T(8,128)} %param.19) | copy-start | bytes 24580
  123.0 15.8 %all-to-all-start.3 = ((bf16[32,16,128]{2,1,0:T(8,128)(2,1)}), bf16[32,16,128]{2,1,0:T(8,128)(2,1)S(1)}, u32[]{:S(2)}, u32[]{:S(2)}) async-start(bf16[32,16,128]{2,1,0:T(8,128)(2,1)} %broadcast_in_dim.90), calls=%async_computation.3 | async-start | bytes 262144 | tf_op jit(solution)/shard_map/all_to_all | solution.py:19
where the time goes:
time: 158 us; the launch traced here: 157 us
  waiting for transfers between devices  58.7 us (37%)
  starting transfers between devices  33.2 us (21%)
  other arithmetic  24.8 us (16%)
  blocking collectives  15.8 us (10%)
  matrix products  15.7 us (10%)
  local copies, waits for them, and re-layouts  7.96 us (5%)
    all_to_all x3, waiting for transfers between devices, from_everyone(): lax.all_to_all(jnp.broadcast_to(x[None], (size, *x.shape)), axis, 0, 0, t...  55.9 us
    all_to_all x3, starting transfers between devices, from_everyone(): lax.all_to_all(jnp.broadcast_to(x[None], (size, *x.shape)), axis, 0, 0, t...  23.7 us
    all_gather x1, blocking collectives, broadcast(): lax.all_gather(x, axis)  15.8 us
    convert_element_type x1, other arithmetic, body(): normalized_input = (stream * lax.rsqrt(meansq + 1e-05) * norm_gain.astype...  10.4 us
    all_to_all x1, starting transfers between devices, sent_and_summed(): pieces = lax.all_to_all(cut_along(x, dim, size), axis, 0, 0, tiled=True)  9.49 us
    dot_general x1, matrix products, body(): jnp.dot(normalized_input, query_weight, preferred_element_type=jnp.float32)  8.16 us
    broadcast_in_dim x3, local copies, waits for them, and re-layouts, from_everyone(): jnp.broadcast_to(x[None], (size, *x.shape))  5.45 us
    reduce_sum x1, other arithmetic, over_copies(): return from_everyone(x, axis).sum(axis=0)  5.26 us
  transfers between devices with their start and end apart: 4, of which 3 were waited for; matrix products, arithmetic and copies ran while one was open for 17% of the time, Pallas kernels for 0%

commit v1 on v0

v1 whole, which is shorter than its diff:
```python
import jax
import jax.numpy as jnp
from jax import lax
from jax.sharding import PartitionSpec as P

LEN = 256


adapter_scale = 0.5
learn_rate = 0.003
beta_one = 0.9
beta_two = 0.999
fix_one = 1.0 - 0.9**10
fix_two = 1.0 - 0.999**10


def core_swap(x):
    size = lax.axis_size("mp")
    return lax.ppermute(x, "mp", [(i, i ^ 1) for i in range(size)])


def chip_shift(x, hops):
    size = lax.axis_size("mp")
    return lax.ppermute(x, "mp", [(i, (i + 2 * hops) % size) for i in range(size)])


def summed_over_mp(partial, core):
    tokens, n = partial.shape
    half = tokens // 2
    chips = lax.axis_size("mp") // 2
    keep = lax.dynamic_slice_in_dim(partial, core * half, half, 0)
    give = lax.dynamic_slice_in_dim(partial, (1 - core) * half, half, 0)
    own = keep + core_swap(give)
    sent = own.astype(jnp.bfloat16)
    hops = sorted(range(1, chips), key=lambda k: -min(k, chips - k))
    total = own
    for k in hops:
        total = total + chip_shift(sent, k).astype(jnp.float32)
    mine = total.astype(jnp.bfloat16)
    other = core_swap(mine)
    low = jnp.where(core == 0, mine, other)
    high = jnp.where(core == 0, other, mine)
    return jnp.concatenate([low, high], axis=0)


def dot_rows(left, right):
    return lax.dot_general(
        left, right, (((0,), (0,)), ((), ())), preferred_element_type=jnp.float32
    )


def dot_columns(left, right):
    return lax.dot_general(
        left, right, (((1,), (1,)), ((), ())), preferred_element_type=jnp.float32
    )


def body(
    resid, norm_gain, query_weight, cotangent, lengths, owner, adapter_table, moment_one, moment_two
):
    n_actor = lax.axis_size("actor")
    n_mp = lax.axis_size("mp")
    mp_index = lax.axis_index("mp")
    actor_index = lax.axis_index("actor")
    core = mp_index % 2
    tokens, width = resid.shape
    cols = query_weight.shape[1]
    block = adapter_table.shape[2]
    rank = adapter_table.shape[3] // 2
    now = adapter_table.reshape(block, 2 * rank).astype(jnp.bfloat16)
    part = lax.all_to_all(
        jnp.broadcast_to(now[None], (n_actor, block, 2 * rank)), "actor", 0, 0, tiled=True
    )
    mine = jnp.take(part, owner, axis=0).reshape(cols, 2 * rank)
    stream = resid.astype(jnp.float32)
    meansq = jnp.mean(stream * stream, axis=1, keepdims=True)
    normed = (
        stream * lax.rsqrt(meansq + 1e-05) * norm_gain.astype(jnp.float32)[None, :]
    ).astype(jnp.bfloat16)
    index = jnp.arange(tokens, dtype=jnp.int32)
    seq_ids = jnp.arange(lengths.shape[0], dtype=jnp.int32)
    live = jnp.any(
        ((index // LEN)[:, None] == seq_ids[None, :])
        & ((index % LEN)[:, None] < lengths[None, :]),
        axis=1,
    )
    masked = jnp.where(live[:, None], cotangent, jnp.zeros_like(cotangent))
    normed_local = lax.dynamic_slice_in_dim(normed, mp_index * cols, cols, 1)
    low_part = jnp.dot(normed_local, mine[:, :rank], preferred_element_type=jnp.float32)
    back_part = jnp.dot(masked, mine[:, rank:], preferred_element_type=jnp.float32)
    both = summed_over_mp(jnp.concatenate([low_part, back_part], axis=1), core)
    low = both[:, :rank]
    back = both[:, rank:]
    base = jnp.dot(normed, query_weight, preferred_element_type=jnp.float32)
    extra = dot_columns(low, mine[:, rank:])
    query = jnp.where(live[:, None], base + adapter_scale * extra, 0.0).astype(jnp.bfloat16)
    grad = adapter_scale * jnp.concatenate(
        [dot_rows(normed_local, back), dot_rows(masked, low)], axis=1
    )
    actors = jnp.arange(n_actor, dtype=jnp.int32)
    inverse = jnp.sum(jnp.where(owner[None, :] == actors[:, None], actors[None, :], 0), axis=1)
    sent = jnp.take(grad.reshape(n_actor, block, 2 * rank), inverse, axis=0)
    summed = lax.all_to_all(sent, "actor", 0, 0, tiled=True).sum(axis=0)
    first = beta_one * moment_one.reshape(block, 2 * rank) + (1.0 - beta_one) * summed
    second = beta_two * moment_two.reshape(block, 2 * rank) + (1.0 - beta_two) * summed * summed
    updated = adapter_table.reshape(block, 2 * rank) - learn_rate * (first / fix_one) / (
        jnp.sqrt(second / fix_two) + 1e-08
    )
    fresh = updated.astype(jnp.bfloat16)
    slices = lax.all_gather(fresh, "mp")
    ratio = n_actor // n_mp
    a_out = jnp.broadcast_to(
        slices[:, None, :, :rank], (n_mp, ratio, block, rank)
    ).reshape(n_actor, block, rank)
    b_out = jnp.broadcast_to(fresh[None, :, rank:], (n_actor, block, rank))
    got = lax.all_to_all(jnp.concatenate([a_out, b_out], axis=2), "actor", 0, 0, tiled=True)
    ordered = jnp.take(got, owner, axis=0).reshape(cols, 2 * rank)
    row_count = width // n_actor
    a_rows = lax.dynamic_slice_in_dim(ordered, actor_index % ratio * row_count, row_count, 0)
    weight_rows = lax.dynamic_slice_in_dim(query_weight, actor_index * row_count, row_count, 0)
    merged = (
        weight_rows.astype(jnp.float32)
        + adapter_scale * dot_columns(a_rows[:, :rank], ordered[:, rank:])
    ).astype(jnp.bfloat16)
    shape = adapter_table.shape
    return (query, updated.reshape(shape), first.reshape(shape), second.reshape(shape), merged)


def solution(mesh):
    return jax.shard_map(
        body,
        mesh=mesh,
        in_specs=(
            P("actor", None),
            P(),
            P(None, "mp"),
            P("actor", "mp"),
            P("actor"),
            P(),
            P("mp", "actor", None, None),
            P("mp", "actor", None, None),
            P("mp", "actor", None, None),
        ),
        out_specs=(
            P("actor", "mp"),
            P("mp", "actor", None, None),
            P("mp", "actor", None, None),
            P("mp", "actor", None, None),
            P("actor", "mp"),
        ),
        check_vma=False,
    )
```

time: 158 us -> 107 us (0.68)
  waiting for transfers between devices: 58.7 us -> 17.4 us
  local copies, waits for them, and re-layouts: 7.96 us -> 2.53 us
  other arithmetic: 24.8 us -> 20.6 us
    all_to_all x4 -> x3, waiting for transfers between devices: 58.7 us -> 11.4 us  [the longest x1 8.23 us: body(): lax.all_to_all(jnp.concatenate([a_out, b_out], axis=2), 'actor', 0, 0, ti...]
    ppermute x0 -> x5, starting transfers between devices: none -> 7.83 us  [the longest x3 5.68 us: chip_shift(): lax.ppermute(x, 'mp', [(i, (i + 2 * hops) % size) for i in range(size)])]
    all_to_all x4 -> x3, starting transfers between devices: 33.2 us -> 26 us  [the longest x1 11.9 us: body(): lax.all_to_all(jnp.broadcast_to(now[None], (n_actor, block, 2 * rank)), '...]
    ppermute x0 -> x5, waiting for transfers between devices: none -> 5.97 us  [the longest x3 3.95 us: chip_shift(): lax.ppermute(x, 'mp', [(i, (i + 2 * hops) % size) for i in range(size)])]
    reduce_sum x2 -> x1, other arithmetic: 5.3 us -> 0.04 us  [body(): summed = lax.all_to_all(sent, 'actor', 0, 0, tiled=True).sum(axis=0)]
    broadcast_in_dim x3, local copies, waits for them, and re-layouts: 5.45 us -> 0.71 us  [the longest x1 0.67 us: body(): jnp.broadcast_to(now[None], (n_actor, block, 2 * rank))]
    convert_element_type x3 -> x6, other arithmetic: 11.1 us -> 11.3 us  [the longest x1 10.4 us: body(): normed = (stream * lax.rsqrt(meansq + 1e-05) * norm_gain.astype(jnp.float...]
  transfers between devices with their start and end apart: 4 -> 8, of which waited for: 3 -> 6; matrix products, arithmetic and copies ran while one was open for 17% -> 25% of each run, Pallas kernels for 0% -> 0%
where the time goes in v1:
time: 107 us
  starting transfers between devices  33.9 us (32%)
  other arithmetic  20.6 us (19%)
  waiting for transfers between devices  17.4 us (16%)
  matrix products  16.1 us (15%)
  blocking collectives  15 us (14%)
  local copies, waits for them, and re-layouts  2.53 us (2%)
    all_gather x1, blocking collectives, body(): slices = lax.all_gather(fresh, 'mp')  15 us
    all_to_all x1, starting transfers between devices, body(): lax.all_to_all(jnp.broadcast_to(now[None], (n_actor, block, 2 * rank)), '...  11.9 us
    convert_element_type x1, other arithmetic, body(): normed = (stream * lax.rsqrt(meansq + 1e-05) * norm_gain.astype(jnp.float...  10.4 us
    all_to_all x1, starting transfers between devices, body(): summed = lax.all_to_all(sent, 'actor', 0, 0, tiled=True).sum(axis=0)  9.68 us
    all_to_all x1, waiting for transfers between devices, body(): lax.all_to_all(jnp.concatenate([a_out, b_out], axis=2), 'actor', 0, 0, ti...  8.23 us
    dot_general x1, matrix products, body(): base = jnp.dot(normed, query_weight, preferred_element_type=jnp.float32)  8.15 us
    ppermute x3, starting transfers between devices, chip_shift(): lax.ppermute(x, 'mp', [(i, (i + 2 * hops) % size) for i in range(size)])  5.68 us
    reduce_sum x1, other arithmetic, body(): meansq = jnp.mean(stream * stream, axis=1, keepdims=True)  5.07 us
  transfers between devices with their start and end apart: 8, of which 6 were waited for; matrix products, arithmetic and copies ran while one was open for 25% of the time, Pallas kernels for 0%

profile of v1, /device:TPU:1, one launch (start us, length us, event | category | flops | bytes accessed | tf_op | source)
XLA Modules:
  0.0 106.5 jit_solution(281984002965692838)
XLA Ops:
  0.6 0.7 bitcast_convert_fusion
  2.0 11.9 %all-to-all-start = ((bf16[32,16,128]{2,1,0:T(8,128)(2,1)}), bf16[32,16,128]{2,1,0:T(8,128)(2,1)S(1)}, u32[]{:S(2)}, u32[]{:S(2)}) async-start(bf16[32,16,128]{2,1,0:T(8,128)(2,1)} %broadcast_in_dim.82), calls=%async_computation | async-start | bytes 262144 | tf_op jit(solution)/shard_map/all_to_all | solution.py:71
  14.5 0.7 convert_element_type.53
  15.2 5.1 %fusion = f32[1024]{0:T(1024)S(1)} fusion(bf16[1024,4096]{1,0:T(8,128)(2,1)} %param.11), kind=kLoop, calls=%fused_computation.5 | loop fusion | flops 12581888 | bytes 8392704 | tf_op jit(solution)/shard_map/reduce_sum | solution.py:76
  20.4 10.4 %fusion.2 = bf16[1024,4096]{1,0:T(8,128)(2,1)} fusion(bf16[1024,4096]{1,0:T(8,128)(2,1)} %param.11, f32[4096]{0:T(1024)S(1)} %convert_element_type.53, f32[1024]{0:T(1024)S(1)} %add_rsqrt_fusion), kind=kLoop, calls=%fused_computation.7 | loop fusion | flops 16777216 | bytes 16797696 | tf_op jit(solution)/shard_map/convert_element_type | solution.py:79
  31.6 1.7 %fusion.7 = f32[1024,64]{0,1:T(8,128)S(1)} fusion(bf16[1024,4096]{1,0:T(8,128)(2,1)} %fusion.2, s32[]{:T(128)S(6)} %select_n.99, bf16[512,128]{1,0:T(8,128)(2,1)S(1)} %bitcast.48), kind=kOutput, calls=%fused_computation.15 | convolution fusion | flops 67108864 | bytes 1441796 | tf_op jit(solution)/shard_map/dot_general | solution.py:89
  33.9 1.0 collective-permute-start
  35.1 1.1 collective-permute-done
  36.2 3.0 %collective-permute-start.1 = (bf16[512,128]{0,1:T(8,128)(2,1)S(1)}, bf16[512,128]{0,1:T(8,128)(2,1)S(1)}, u32[]{:S(2)}, u32[]{:S(2)}) collective-permute-start(bf16[512,128]{0,1:T(8,128)(2,1)S(1)} %get-tuple-element.9), channel_id=1, source_target_pairs={{0,4},{1,5},{2,6},{3,7},{4,0},{5,1},{6,2},{7,3},{8,12},{9,13},{10,... | collective-permute-start | bytes 393224 | tf_op jit(solution)/shard_map/ppermute | solution.py:24
  39.6 2.3 %collective-permute-start.3 = (bf16[512,128]{0,1:T(8,128)(2,1)S(1)}, bf16[512,128]{0,1:T(8,128)(2,1)S(1)}, u32[]{:S(2)}, u32[]{:S(2)}) collective-permute-start(bf16[512,128]{0,1:T(8,128)(2,1)S(1)} %get-tuple-element.9), channel_id=1, source_target_pairs={{0,6},{1,7},{2,0},{3,1},{4,2},{5,3},{6,4},{7,5},{8,14},{9,15},{10,... | collective-permute-start | bytes 393224 | tf_op jit(solution)/shard_map/ppermute | solution.py:24
  42.5 3.4 %collective-permute-done.2 = bf16[512,128]{0,1:T(8,128)(2,1)S(1)} collective-permute-done((bf16[512,128]{0,1:T(8,128)(2,1)S(1)}, bf16[512,128]{0,1:T(8,128)(2,1)S(1)}, u32[]{:S(2)}, u32[]{:S(2)}) %collective-permute-start.2) | collective-permute-done | bytes 131104 | tf_op jit(solution)/shard_map/ppermute | solution.py:24
  45.9 1.1 %collective-permute-start.4 = (bf16[512,128]{0,1:T(8,128)(2,1)S(1)}, bf16[512,128]{0,1:T(8,128)(2,1)S(1)}, u32[]{:S(2)}, u32[]{:S(2)}) collective-permute-start(bf16[512,128]{0,1:T(8,128)(2,1)S(1)} %add_convert_fusion), channel_id=1, source_target_pairs={{0,1},{1,0},{2,3},{3,2},{4,5},{5,4},{6,7},{7,6},{8,9},{9,8},{10,11... | collective-permute-start | bytes 393224 | tf_op jit(solution)/shard_map/ppermute | solution.py:19
  47.0 1.0 collective-permute-done.4
  48.0 1.7 %fusion.5 = f32[512,64]{1,0:T(8,128)S(1)} fusion(bf16[1024,4096]{1,0:T(8,128)(2,1)} %fusion.2, s32[]{:T(128)S(6)} %select_n.99, bf16[512,128]{0,1:T(8,128)(2,1)S(1)} %get-tuple-element.11, bf16[512,128]{0,1:T(8,128)(2,1)S(1)} %get-tuple-element.12), kind=kOutput, calls=%fused_computation.13 | convolution fusion | flops 67371008 | bytes 1441796 | tf_op jit(solution)/shard_map/dot_general | solution.py:47
  51.1 0.8 broadcast_select_fusion.3
  52.0 9.7 %all-to-all-start.1 = ((f32[32,16,128]{2,1,0:T(8,128)}), f32[32,16,128]{2,1,0:T(8,128)S(1)}, u32[]{:S(2)}, u32[]{:S(2)}) async-start(f32[32,16,128]{2,1,0:T(8,128)} %broadcast_select_fusion.3), calls=%async_computation.1 | async-start | bytes 524288 | tf_op jit(solution)/shard_map/all_to_all | solution.py:103
  61.7 8.2 %fusion.60 = f32[1024,512]{1,0:T(8,128)S(1)} fusion(bf16[1024,4096]{1,0:T(8,128)(2,1)} %fusion.2, bf16[4096,512]{1,0:T(8,128)(2,1)} %param.13), kind=kOutput, calls=%fused_computation.105 | convolution fusion | flops 4294967296 | bytes 14680064 | tf_op jit(solution)/shard_map/dot_general | solution.py:94
  69.9 3.2 %all-to-all-done.1 = f32[32,16,128]{2,1,0:T(8,128)S(1)} async-done(((f32[32,16,128]{2,1,0:T(8,128)}), f32[32,16,128]{2,1,0:T(8,128)S(1)}, u32[]{:S(2)}, u32[]{:S(2)}) %all-to-all-start.1) | async-done | bytes 262176 | tf_op jit(solution)/shard_map/all_to_all | solution.py:103
  73.8 15.0 %all_gather.4 = bf16[8,16,128]{2,1,0:T(8,128)(2,1)S(1)} all-gather(bf16[1,16,128]{2,1,0:T(8,128)(2,1)S(1)} %fusion.43), channel_id=1, replica_groups=mesh['actor'=32,'mp'=8] {'mp'}, dimensions={0}, use_global_device_ids=true | all-gather | bytes 36864 | tf_op jit(solution)/shard_map/all_gather | solution.py:110
  89.0 0.8 pad_maximum_fusion.2
  89.7 4.5 %all-to-all-start.2 = ((bf16[32,16,128]{2,1,0:T(8,128)(2,1)}), bf16[32,16,128]{2,1,0:T(8,128)(2,1)S(1)}, u32[]{:S(2)}, u32[]{:S(2)}) async-start(bf16[32,16,128]{2,1,0:T(8,128)(2,1)} %pad_maximum_fusion.2), calls=%async_computation.2 | async-start | bytes 262144 | tf_op jit(solution)/shard_map/all_to_all | solution.py:116
  94.2 1.5 %select_convert_fusion = bf16[1024,512]{1,0:T(8,128)(2,1)} fusion(f32[1024,512]{1,0:T(8,128)S(1)} %fusion.60, pred[1024]{0:T(1024)(128)(4,1)S(1)} %fusion.22, bf16[512,128]{1,0:T(8,128)(2,1)S(1)} %bitcast.50, bf16[512,128]{0,1:T(8,128)(2,1)S(1)} %get-tuple-element.12, bf16[512,128]{0,1:T(8,128)(2,1)S(1)} %get-tuple-element.11), kind=kOutput, calls=%fused_computation.8 | convolution fusion | flops 69468160 | bytes 3539968 | tf_op jit(solution)/shard_map/dot_general | solution.py:53
  95.7 8.2 %all-to-all-done.2 = bf16[32,16,128]{2,1,0:T(8,128)(2,1)S(1)} async-done(((bf16[32,16,128]{2,1,0:T(8,128)(2,1)}), bf16[32,16,128]{2,1,0:T(8,128)(2,1)S(1)}, u32[]{:S(2)}, u32[]{:S(2)}) %all-to-all-start.2) | async-done | bytes 131104 | tf_op jit(solution)/shard_map/all_to_all | solution.py:116
  104.7 1.8 %fusion.4 = bf16[128,512]{1,0:T(8,128)(2,1)} fusion(bf16[512,128]{1,0:T(8,128)(2,1)S(1)} %bitcast.53, bf16[4096,512]{1,0:T(8,128)(2,1)} %param.13, s32[]{:T(128)S(6)} %select_n.110, s32[]{:T(128)S(6)} %select_n.112), kind=kOutput, calls=%fused_computation.11 | convolution fusion | flops 8650752 | bytes 425992 | tf_op jit(solution)/shard_map/dot_general | solution.py:53
  (46 shorter events, 6.9 us)
Async XLA Ops:
  2.0 28.9 %all-to-all-start = ((bf16[32,16,128]{2,1,0:T(8,128)(2,1)}), bf16[32,16,128]{2,1,0:T(8,128)(2,1)S(1)}, u32[]{:S(2)}, u32[]{:S(2)}) async-start(bf16[32,16,128]{2,1,0:T(8,128)(2,1)} %broadcast_in_dim.82), calls=%async_computation | async-start | bytes 262144 | tf_op jit(solution)/shard_map/all_to_all | solution.py:71
  20.3 10.5 %copy-start.3 = (s32[4]{0:T(128)S(1)}, s32[4]{0:T(128)}, u32[]{:S(2)}) copy-start(s32[4]{0:T(128)} %param.15) | copy-start | bytes 52
  20.3 10.6 %copy-start.5 = (s32[32]{0:T(128)S(1)}, s32[32]{0:T(128)}, u32[]{:S(2)}) copy-start(s32[32]{0:T(128)} %param.16) | copy-start | bytes 388
  20.3 13.0 %copy-start.4 = (bf16[1024,512]{1,0:T(8,128)(2,1)S(1)}, bf16[1024,512]{1,0:T(8,128)(2,1)}, u32[]{:S(2)}) copy-start(bf16[1024,512]{1,0:T(8,128)(2,1)} %param.14) | copy-start | bytes 3145732
  33.9 2.2 %collective-permute-start = (f32[512,128]{0,1:T(8,128)S(1)}, f32[512,128]{0,1:T(8,128)S(1)}, u32[]{:S(2)}, u32[]{:S(2)}) collective-permute-start(f32[512,128]{0,1:T(8,128)S(1)} %fusion.11), channel_id=1, source_target_pairs={{0,1},{1,0},{2,3},{3,2},{4,5},{5,4},{6,7},{7,6},{8,9},{9,8},{10,11... | collective-permute-start | bytes 786440 | tf_op jit(solution)/shard_map/ppermute | solution.py:19
  36.2 6.3 %collective-permute-start.1 = (bf16[512,128]{0,1:T(8,128)(2,1)S(1)}, bf16[512,128]{0,1:T(8,128)(2,1)S(1)}, u32[]{:S(2)}, u32[]{:S(2)}) collective-permute-start(bf16[512,128]{0,1:T(8,128)(2,1)S(1)} %get-tuple-element.9), channel_id=1, source_target_pairs={{0,4},{1,5},{2,6},{3,7},{4,0},{5,1},{6,2},{7,3},{8,12},{9,13},{10,... | collective-permute-start | bytes 393224 | tf_op jit(solution)/shard_map/ppermute | solution.py:24
  39.2 6.6 %collective-permute-start.2 = (bf16[512,128]{0,1:T(8,128)(2,1)S(1)}, bf16[512,128]{0,1:T(8,128)(2,1)S(1)}, u32[]{:S(2)}, u32[]{:S(2)}) collective-permute-start(bf16[512,128]{0,1:T(8,128)(2,1)S(1)} %get-tuple-element.9), channel_id=1, source_target_pairs={{0,2},{1,3},{2,4},{3,5},{4,6},{5,7},{6,0},{7,1},{8,10},{9,11},{10,... | collective-permute-start | bytes 393224 | tf_op jit(solution)/shard_map/ppermute | solution.py:24
  39.6 6.2 %collective-permute-start.3 = (bf16[512,128]{0,1:T(8,128)(2,1)S(1)}, bf16[512,128]{0,1:T(8,128)(2,1)S(1)}, u32[]{:S(2)}, u32[]{:S(2)}) collective-permute-start(bf16[512,128]{0,1:T(8,128)(2,1)S(1)} %get-tuple-element.9), channel_id=1, source_target_pairs={{0,6},{1,7},{2,0},{3,1},{4,2},{5,3},{6,4},{7,5},{8,14},{9,15},{10,... | collective-permute-start | bytes 393224 | tf_op jit(solution)/shard_map/ppermute | solution.py:24
  45.9 2.1 %collective-permute-start.4 = (bf16[512,128]{0,1:T(8,128)(2,1)S(1)}, bf16[512,128]{0,1:T(8,128)(2,1)S(1)}, u32[]{:S(2)}, u32[]{:S(2)}) collective-permute-start(bf16[512,128]{0,1:T(8,128)(2,1)S(1)} %add_convert_fusion), channel_id=1, source_target_pairs={{0,1},{1,0},{2,3},{3,2},{4,5},{5,4},{6,7},{7,6},{8,9},{9,8},{10,11... | collective-permute-start | bytes 393224 | tf_op jit(solution)/shard_map/ppermute | solution.py:19
  52.0 21.1 %all-to-all-start.1 = ((f32[32,16,128]{2,1,0:T(8,128)}), f32[32,16,128]{2,1,0:T(8,128)S(1)}, u32[]{:S(2)}, u32[]{:S(2)}) async-start(f32[32,16,128]{2,1,0:T(8,128)} %broadcast_select_fusion.3), calls=%async_computation.1 | async-start | bytes 524288 | tf_op jit(solution)/shard_map/all_to_all | solution.py:103
  61.6 11.5 %copy-start.1 = (f32[1,1,16,128]{3,2,1,0:T(8,128)S(1)}, f32[1,1,16,128]{3,2,1,0:T(8,128)}, u32[]{:S(2)}) copy-start(f32[1,1,16,128]{3,2,1,0:T(8,128)} %param.19) | copy-start | bytes 24580
  61.7 11.5 %copy-start = (f32[1,1,16,128]{3,2,1,0:T(8,128)S(1)}, f32[1,1,16,128]{3,2,1,0:T(8,128)}, u32[]{:S(2)}) copy-start(f32[1,1,16,128]{3,2,1,0:T(8,128)} %param.17) | copy-start | bytes 24580
  61.7 11.5 %copy-start.2 = (f32[1,1,16,128]{3,2,1,0:T(8,128)S(1)}, f32[1,1,16,128]{3,2,1,0:T(8,128)}, u32[]{:S(2)}) copy-start(f32[1,1,16,128]{3,2,1,0:T(8,128)} %param.18) | copy-start | bytes 24580
  89.7 14.2 %all-to-all-start.2 = ((bf16[32,16,128]{2,1,0:T(8,128)(2,1)}), bf16[32,16,128]{2,1,0:T(8,128)(2,1)S(1)}, u32[]{:S(2)}, u32[]{:S(2)}) async-start(bf16[32,16,128]{2,1,0:T(8,128)(2,1)} %pad_maximum_fusion.2), calls=%async_computation.2 | async-start | bytes 262144 | tf_op jit(solution)/shard_map/all_to_all | solution.py:116
